TPU v7x, 256 devices: a whole 4x4x8 slice. The times are simulated.
256 devices in a mesh: basis: 32 (over z, x_lo, core), band: 8 (over x_hi, y).
Axes of the slice: x: 4 (x_hi: 2, x_lo: 2; x = x_hi * 2 + x_lo), y: 4, z: 8, core: 2. Of those that a mesh axis runs over, the one named last changes fastest.
Arguments:
- matching: bfloat16 [162, 81920], P(None, 'basis'), may hold values from -6 to 6
- vectors: bfloat16 [81920, 16384], P('basis', 'band'), may hold values from -0.01953125 to 0.01953125
- weights: float32 [16384], P('band'), may hold values from 1.2207031e-05 to 0.00012207031
- gaunt_index: int32 [3, 4096], replicated, may hold values from 0 to 80
- gaunt_value: float32 [4096], replicated, may hold values from -4 to 4
Outputs:
- density_matrix: float32 [162, 162], replicated
- density: float32 [4, 81], replicated
All inputs are finite; a program needn't handle non-finite values.
Results may differ from a plain program's by a relative error of at most 0.0003.
Values sent between devices are 32-bit elements; how exact they have to be, the bound alone decides.
A program may use at most 64 MiB of HBM per device.

v0:
```python
import jax
import jax.numpy as jnp
from jax import lax
from jax.sharding import Mesh
from jax.sharding import PartitionSpec as P

BASIS = ("basis_0", "basis_1", "basis_2")


def split_up(shard, dim, length):
    before, after = (shard.shape[:dim], shard.shape[dim + 1 :])
    return jnp.moveaxis(shard.reshape(*before, length, -1, *after), dim, 0)


def summed_on_arrival(shard, axis, dim):
    pieces = split_up(shard, dim, lax.axis_size(axis))
    arrived = lax.all_to_all(pieces, axis, split_axis=0, concat_axis=0, tiled=True)
    return arrived.sum(axis=0)


def sum_by_axis(shard, axes, dim):
    far, near = axes
    pieces = split_up(shard, dim, lax.axis_size(far))
    nearer = summed_on_arrival(pieces, near, dim + 1)
    arrived = lax.all_to_all(nearer, far, split_axis=0, concat_axis=0, tiled=True)
    return arrived.sum(axis=0)


def padded_to(lines, length):
    spare = -len(lines) % length
    return jnp.pad(lines, [(0, spare)] + [(0, 0)] * (lines.ndim - 1))


def sent_to_all(shard, axis):
    copies = jnp.broadcast_to(shard, (lax.axis_size(axis), *shard.shape))
    return lax.all_to_all(copies, axis, split_axis=0, concat_axis=0, tiled=True)


def joined_along(pieces, dim):
    shape = list(pieces.shape[1:])
    shape[dim] *= pieces.shape[0]
    return jnp.moveaxis(pieces, 0, dim).reshape(shape)


def whole_of(shard, axes, dim):
    far, near = axes
    leading = sent_to_all(shard, far)
    pieces = jnp.swapaxes(sent_to_all(leading, near), 0, 1)
    return joined_along(pieces.reshape(-1, *shard.shape), dim)


def total_of(shard, axes):
    lines = shard.reshape(-1)
    own = sum_by_axis(padded_to(lines, lax.axis_size(axes[0]) * lax.axis_size(axes[1])), axes, 0)
    whole = whole_of(own, axes, 0)
    return whole[: len(lines)].reshape(shard.shape)


def of_everyone(shard, axis):
    everything = sent_to_all(shard, axis)
    return jnp.sum(everything, axis=0)


def weighted_pairs(coeffs, band_weights):
    scaled = coeffs * band_weights[None, :]
    return lax.dot_general(
        scaled,
        coeffs,
        (((1,), (1,)), ((), ())),
        precision=lax.Precision.HIGHEST,
        preferred_element_type=jnp.float32,
    )


def gaunt_density(density_matrix, gaunt_index, gaunt_value):
    harmonics = density_matrix.shape[0] // 2
    codes = jnp.arange(harmonics, dtype=jnp.int32)[:, None]
    first_table = (gaunt_index[0][None, :] == codes).astype(jnp.float32)
    second_table = (gaunt_index[1][None, :] == codes).astype(jnp.float32)
    target_table = (gaunt_index[2][None, :] == codes).astype(jnp.float32)
    collected = []
    for radial in range(2):
        for other in range(2):
            block = density_matrix[
                radial * harmonics : (radial + 1) * harmonics,
                other * harmonics : (other + 1) * harmonics,
            ]
            spread = jnp.dot(
                block,
                second_table,
                precision=lax.Precision.HIGHEST,
                preferred_element_type=jnp.float32,
            )
            picked = jnp.sum(spread * first_table, axis=0)
            collected.append(picked * gaunt_value)
    values = jnp.stack(collected)
    return lax.dot_general(
        values,
        target_table,
        (((1,), (1,)), ((), ())),
        precision=lax.Precision.HIGHEST,
        preferred_element_type=jnp.float32,
    )


def body(matching, vectors, weights, gaunt_index, gaunt_value):
    partial_value = jnp.dot(matching, vectors, preferred_element_type=jnp.float32)
    summed = total_of(partial_value, (("basis_0", "basis_1"), "basis_2"))
    local_terms = weighted_pairs(summed, weights)
    density_matrix = of_everyone(local_terms, "band")
    density = gaunt_density(density_matrix, gaunt_index, gaunt_value)
    return (density_matrix, density)


def solution(mesh):
    finer = Mesh(
        mesh.devices.reshape(8, 2, 2, mesh.shape["band"]), ("basis_0", "basis_1", "basis_2", "band")
    )
    return jax.shard_map(
        body,
        mesh=finer,
        in_specs=(P(None, BASIS), P(BASIS, "band"), P("band"), P(), P()),
        out_specs=(P(), P()),
        check_vma=False,
    )
```

profile of v0, /device:TPU:1, one launch (start us, length us, event | category | flops | bytes accessed | tf_op | source)
XLA Modules:
  0.0 120.6 jit_solution(8115568189475792363)
XLA Ops:
  0.6 0.0 copy-start
  0.6 1.1 copy-done
  1.8 5.9 %fusion.25 = f32[162,2048]{1,0:T(8,128)S(1)} fusion(bf16[162,2560]{1,0:T(8,128)(2,1)S(1)} %copy-done, bf16[2560,2048]{1,0:T(8,128)(2,1)} %param.6), kind=kOutput, calls=%fused_computation.35 | convolution fusion | flops 1698693120 | bytes 12642304 | tf_op jit(solution)/shard_map/dot_general | solution.py:107
  7.7 2.1 %reshape_reshape.3 = f32[16,2,10368]{2,1,0:T(2,128)} reshape(f32[162,2048]{1,0:T(8,128)S(1)} %fusion.25) | data formatting | bytes 2654208 | tf_op jit(solution)/shard_map/reshape;reshape | solution.py:12
  9.8 1.4 %copy.22 = f32[16,2,10368]{2,0,1:T(8,128)S(1)} copy(f32[16,2,10368]{2,1,0:T(2,128)} %reshape_reshape.3) | data formatting | bytes 2654208 | tf_op jit(solution)/shard_map/reshape;reshape | solution.py:12
  11.2 7.6 %all_to_all.33 = f32[2,16,10368]{2,1,0:T(8,128)S(1)} all-to-all(f32[2,16,10368]{2,1,0:T(8,128)S(1)} %bitcast.22), channel_id=1, replica_groups=mesh['basis_0'=8,'basis_1'=2,'basis_2'=2,'band'=8] {'basis_2'}, dimensions={0} | all-to-all | bytes 2654208 | tf_op jit(solution)/shard_map/all_to_all | solution.py:17
  18.8 0.1 reduce_sum.63
  19.0 0.5 all_to_all.22
  19.5 27.2 %all_to_all.34 = f32[16,1,10368]{2,1,0:T(1,128)S(1)} all-to-all(f32[16,1,10368]{2,1,0:T(1,128)S(1)} %all_to_all.22), channel_id=1, replica_groups=mesh['basis_0'=8,'basis_1'=2,'basis_2'=2,'band'=8] {'basis_0','basis_1'}, dimensions={0} | all-to-all | bytes 1327104 | tf_op jit(solution)/shard_map/all_to_all | solution.py:25
  46.7 0.0 copy-start.6
  46.7 0.4 reduce_sum.64
  47.1 1.2 broadcast_in_dim.11
  48.3 3.6 %all-to-all-start.2 = ((f32[16,1,10368]{2,1,0:T(1,128)}), f32[16,1,10368]{2,1,0:T(1,128)S(1)}, u32[]{:S(2)}, u32[]{:S(2)}) async-start(f32[16,1,10368]{2,1,0:T(1,128)} %broadcast_in_dim.11), calls=%async_computation.2 | async-start | bytes 1327104 | tf_op jit(solution)/shard_map/all_to_all | solution.py:36
  51.9 0.0 copy-done.6
  51.9 0.1 mul.37
  52.1 2.1 %mul.38 = f32[16,2,10368]{2,1,0:T(2,128)} reshape(f32[162,2048]{1,0:T(8,128)S(1)} %mul.37) | data formatting | bytes 2654208 | tf_op jit(solution)/shard_map/mul | solution.py:65
  54.2 15.5 %all-to-all-done.2 = f32[16,1,10368]{2,1,0:T(1,128)S(1)} async-done(((f32[16,1,10368]{2,1,0:T(1,128)}), f32[16,1,10368]{2,1,0:T(1,128)S(1)}, u32[]{:S(2)}, u32[]{:S(2)}) %all-to-all-start.2) | async-done | bytes 663584 | tf_op jit(solution)/shard_map/all_to_all | solution.py:36
  69.8 0.1 broadcast_in_dim.12
  69.9 0.0 copy-start.2
  69.9 8.5 %all_to_all.35 = f32[2,16,10368]{2,1,0:T(8,128)S(1)} all-to-all(f32[2,16,10368]{2,1,0:T(8,128)S(1)} %broadcast_in_dim.12), channel_id=1, replica_groups=mesh['basis_0'=8,'basis_1'=2,'basis_2'=2,'band'=8] {'basis_2'}, dimensions={0} | all-to-all | bytes 2654208 | tf_op jit(solution)/shard_map/all_to_all | solution.py:36
  78.3 0.0 copy-done.2
  78.3 0.9 fusion.22
  79.3 2.1 %mul.40 = f32[162,2048]{1,0:T(8,128)} reshape(f32[16,2,10368]{2,1,0:T(2,128)S(1)} %fusion.22) | data formatting | bytes 2654208 | tf_op jit(solution)/shard_map/mul | solution.py:65
  81.4 1.8 %copy.21 = f32[2,16,10368]{2,0,1:T(2,128)} copy(f32[2,16,10368]{2,1,0:T(8,128)S(1)} %all_to_all.35) | data formatting | bytes 2654208 | tf_op jit(solution)/shard_map/all_to_all | solution.py:36
  83.2 0.0 copy-start.1
  83.2 3.6 %reshape_reshape_reshape.3 = f32[162,2048]{1,0:T(8,128)} reshape(f32[16,2,10368]{2,1,0:T(2,128)} %bitcast.23) | data formatting | bytes 2654208 | tf_op jit(solution)/shard_map/reshape;reshape;reshape | solution.py:56
  86.8 0.0 copy-done.1
  86.8 2.6 %fusion.26 = f32[162,162]{1,0:T(8,128)S(1)} fusion(f32[162,2048]{1,0:T(8,128)S(1)} %copy-done.1, f32[162,2048]{1,0:T(8,128)} %reshape_reshape_reshape.3), kind=kOutput, calls=%fused_computation.36 | convolution fusion | flops 644972544 | bytes 2759184 | tf_op jit(solution)/shard_map/dot_general | solution.py:66
  89.4 1.2 broadcast_in_dim.13
  90.6 0.0 copy-start.4
  90.6 6.5 %all-to-all-start.4 = ((f32[8,162,162]{2,1,0:T(8,128)}), f32[8,162,162]{2,1,0:T(8,128)S(1)}, u32[]{:S(2)}, u32[]{:S(2)}) async-start(f32[8,162,162]{2,1,0:T(8,128)} %broadcast_in_dim.13), calls=%async_computation.4 | async-start | bytes 2752512 | tf_op jit(solution)/shard_map/all_to_all | solution.py:36
  97.1 0.0 copy-done.4
  97.1 18.1 %all-to-all-done.4 = f32[8,162,162]{2,1,0:T(8,128)S(1)} async-done(((f32[8,162,162]{2,1,0:T(8,128)}), f32[8,162,162]{2,1,0:T(8,128)S(1)}, u32[]{:S(2)}, u32[]{:S(2)}) %all-to-all-start.4) | async-done | bytes 839840 | tf_op jit(solution)/shard_map/all_to_all | solution.py:36
  115.3 0.1 reduce_sum.65
  115.4 0.0 copy-start.3
  115.4 0.9 fusion.3
  116.3 0.9 fusion.4
  117.3 0.0 copy-start.5
  117.3 0.9 fusion.2
  118.2 0.0 copy-done.3
  118.2 0.9 fusion.1
  119.1 0.0 copy-done.5
  119.2 1.4 %fusion = f32[4,81]{1,0:T(4,128)} fusion(s32[4096]{0:T(1024)S(1)} %bitcast.29, f32[1,4096]{1,0:T(1,128)S(1)} %bitcast.27, f32[1,4096]{1,0:T(1,128)S(1)} %bitcast.28, f32[1,4096]{1,0:T(1,128)S(1)} %bitcast.26, f32[1,4096]{1,0:T(1,128)S(1)} %bitcast.25), kind=kOutput, calls=%fused_computation.7 | convolution fusion | flops 16306176 | bytes 83216 | tf_op jit(solution)/shard_map/dot_general | solution.py:97
  (3 shorter events, 0.1 us)
Async XLA Ops:
  0.6 1.2 copy-start
  46.7 5.2 %copy-start.6 = (f32[2048]{0:T(1024)S(1)}, f32[2048]{0:T(1024)}, u32[]{:S(2)}) copy-start(f32[2048]{0:T(1024)} %param.7) | copy-start | bytes 24580
  48.3 21.4 %all-to-all-start.2 = ((f32[16,1,10368]{2,1,0:T(1,128)}), f32[16,1,10368]{2,1,0:T(1,128)S(1)}, u32[]{:S(2)}, u32[]{:S(2)}) async-start(f32[16,1,10368]{2,1,0:T(1,128)} %broadcast_in_dim.11), calls=%async_computation.2 | async-start | bytes 1327104 | tf_op jit(solution)/shard_map/all_to_all | solution.py:36
  69.9 8.5 %copy-start.2 = (f32[16,2,10368]{2,1,0:T(2,128)S(1)}, f32[16,2,10368]{2,1,0:T(2,128)}, u32[]{:S(2)}) copy-start(f32[16,2,10368]{2,1,0:T(2,128)} %mul.38) | copy-start | bytes 3981316
  83.2 3.6 %copy-start.1 = (f32[162,2048]{1,0:T(8,128)S(1)}, f32[162,2048]{1,0:T(8,128)}, u32[]{:S(2)}) copy-start(f32[162,2048]{1,0:T(8,128)} %mul.40) | copy-start | bytes 3981316
  90.6 6.5 %copy-start.4 = (s32[3,4096]{1,0:T(4,128)S(1)}, s32[3,4096]{1,0:T(4,128)}, u32[]{:S(2)}) copy-start(s32[3,4096]{1,0:T(4,128)} %param.8) | copy-start | bytes 147460
  90.6 24.7 %all-to-all-start.4 = ((f32[8,162,162]{2,1,0:T(8,128)}), f32[8,162,162]{2,1,0:T(8,128)S(1)}, u32[]{:S(2)}, u32[]{:S(2)}) async-start(f32[8,162,162]{2,1,0:T(8,128)} %broadcast_in_dim.13), calls=%async_computation.4 | async-start | bytes 2752512 | tf_op jit(solution)/shard_map/all_to_all | solution.py:36
  115.4 2.8 %copy-start.3 = (f32[162,162]{1,0:T(8,128)}, f32[162,162]{1,0:T(8,128)S(1)}, u32[]{:S(2)}) copy-start(f32[162,162]{1,0:T(8,128)S(1)} %reduce_sum.65) | copy-start | bytes 314932
  117.3 1.9 %copy-start.5 = (f32[4096]{0:T(1024)S(1)}, f32[4096]{0:T(1024)}, u32[]{:S(2)}) copy-start(f32[4096]{0:T(1024)} %param.9) | copy-start | bytes 49156
where the time goes:
time: 121 us
  blocking collectives  43.3 us (36%)
  waiting for transfers between devices  33.7 us (28%)
  local copies, waits for them, and re-layouts  17.4 us (14%)
  matrix products  13.6 us (11%)
  starting transfers between devices  10.1 us (8%)
  other arithmetic  1.61 us (1%)
    all_to_all x2, waiting for transfers between devices, sent_to_all(): return lax.all_to_all(copies, axis, split_axis=0, concat_axis=0, tiled=True)  33.7 us
    all_to_all x1, blocking collectives, sum_by_axis(): lax.all_to_all(nearer, far, split_axis=0, concat_axis=0, tiled=True)  27.2 us
    all_to_all x2, starting transfers between devices, sent_to_all(): return lax.all_to_all(copies, axis, split_axis=0, concat_axis=0, tiled=True)  10.1 us
    all_to_all x1, blocking collectives, sent_to_all(): return lax.all_to_all(copies, axis, split_axis=0, concat_axis=0, tiled=True)  8.46 us
    all_to_all x1, blocking collectives, summed_on_arrival(): lax.all_to_all(pieces, axis, split_axis=0, concat_axis=0, tiled=True)  7.6 us
    dot_general x1, matrix products, body(): jnp.dot(matching, vectors, preferred_element_type=jnp.float32)  5.93 us
    mul x3, local copies, waits for them, and re-layouts, weighted_pairs(): scaled = coeffs * band_weights[None, :]  4.38 us
    dot_general x4, matrix products, gaunt_density(): jnp.dot(block, second_table, precision=lax.Precision.HIGHEST, preferred_e...  3.7 us
  transfers between devices with their start and end apart: 2, of which 2 were waited for; matrix products, arithmetic and copies ran while one was open for 2% of the time, Pallas kernels for 0%

commit v1 on v0

v1 whole, which is shorter than its diff:
```python
import jax
import jax.numpy as jnp
from jax import lax
from jax.experimental import pallas as pl
from jax.experimental.pallas import tpu as pltpu
from jax.sharding import PartitionSpec as P

CH = 162
ROWS = 168
HALF = 88
SHIFT = 80
Z = 8
X = 4
Y = 4
LANES = 128
TILES = 32
OFFSETS = (4, 3, 5, 2, 6, 1, 7, 0)
PLANE = tuple((dx, dy) for dx in (2, 1, 3, 0) for dy in (2, 1, 3, 0))
MESH = pl.DeviceIdType.MESH
F32 = jnp.float32


def place(x, y, z, core):
    return {
        "basis": (z * 2 + lax.rem(x, 2)) * 2 + core,
        "band": lax.div(x, 2) * Y + y,
    }


def kernel(
    a_hbm, v_hbm, w_ref, out_ref,
    a_buf, v_buf, part, core_in, pair, x_in, z_out, z_in, full, terms, plane_in,
    own_tile, line_in, tiles,
    a_sem, v_sem, core_s, core_r, x_s, x_r, z_s, z_r, full_s, full_r,
    plane_s, plane_r, line_s, line_r, all_s, all_r,
):
    basis, band = lax.axis_index("basis"), lax.axis_index("band")
    z, xl, core = lax.div(basis, 4), lax.rem(lax.div(basis, 2), 2), lax.rem(basis, 2)
    x, y = lax.div(band, Y) * 2 + xl, lax.rem(band, Y)
    other = 1 - core

    a_copy = pltpu.make_async_copy(a_hbm, a_buf, a_sem)
    a_copy.start()
    targets = [lax.rem(z + off, Z) for off in OFFSETS]
    v_copies = []
    for s in range(Z):
        columns = pl.ds(pl.multiple_of(targets[s] * 256, 256), 256)
        v_copies.append(pltpu.make_async_copy(v_hbm.at[:, columns], v_buf.at[s], v_sem.at[s]))
        v_copies[s].start()

    plane = [
        (place(lax.rem(x + dx, X), lax.rem(y + dy, Y), z, c), dx, dy, flip)
        for dx, dy in PLANE
        for flip, c in ((0, core), (1, other))
        if (dx, dy, flip) != (0, 0, 0)
    ]
    line = [place(x, y, lax.rem(z + dz, Z), core) for dz in range(1, Z)]
    barrier = pltpu.get_barrier_semaphore()
    for device, *_ in plane:
        pl.semaphore_signal(barrier, inc=1, device_id=device, device_id_type=MESH)
    for device in line:
        pl.semaphore_signal(barrier, inc=1, device_id=device, device_id_type=MESH)

    for s in range(Z):
        for h in range(2):
            part[s, h, SHIFT * 2 : ROWS, :] = jnp.zeros((ROWS - SHIFT * 2, LANES), F32)
    full[ROWS:256, :] = jnp.zeros((256 - ROWS, LANES), F32)
    terms[26:TILES] = jnp.zeros((TILES - 26, 8, LANES), F32)

    core_peer = place(x, y, z, other)
    x_peer = place(x + 1 - 2 * xl, y, z, core)

    def remote(src, dst, send, recv, device):
        return pltpu.make_async_remote_copy(
            src_ref=src, dst_ref=dst, send_sem=send, recv_sem=recv,
            device_id=device, device_id_type=MESH,
        )

    mine = pl.ds(pl.multiple_of(SHIFT * core, 8), HALF)
    theirs = pl.ds(pl.multiple_of(SHIFT * other, 8), HALF)
    core_copies, x_copies, z_copies = [], [], []

    def multiply(s):
        v_copies[s].wait()
        product = jnp.dot(a_buf[...], v_buf[s], preferred_element_type=F32)
        part[s, 0, 0:CH, :] = product[:, :LANES]
        part[s, 1, 0:CH, :] = product[:, LANES:]

    def to_core(s):
        copy = remote(part.at[s, :, theirs, :], core_in.at[s], core_s.at[s], core_r.at[s], core_peer)
        copy.start()
        core_copies.append(copy)

    def to_x(s):
        core_copies[s].wait_recv()
        pair[s] = part[s, :, mine, :] + core_in[s]
        copy = remote(pair.at[s, 1 - xl], x_in.at[s], x_s.at[s], x_r.at[s], x_peer)
        copy.start()
        x_copies.append(copy)

    def to_z(s):
        x_copies[s].wait_recv()
        total = pair[s, xl] + x_in[s]
        z_out[s] = total
        if OFFSETS[s]:
            copy = remote(
                z_out.at[s], z_in.at[s], z_s.at[s], z_r.at[s], place(x, y, targets[s], core)
            )
            copy.start()
            z_copies.append(copy)

    a_copy.wait()
    multiply(0)
    pl.semaphore_wait(barrier, len(plane) + len(line))
    to_core(0)
    for s in range(1, Z):
        multiply(s)
        to_core(s)
        if s >= 3:
            to_x(s - 3)
    for s in range(Z - 3, Z):
        to_x(s)
    for s in range(Z):
        to_z(s)
    total = z_out[Z - 1]
    for s in range(Z - 1):
        z_copies[s].wait_recv()
        total = total + z_in[s]

    full[mine, :] = total
    sent = pl.ds(pl.multiple_of(HALF * core, 8), SHIFT)
    full_copy = remote(full.at[sent, :], full.at[sent, :], full_s, full_r, core_peer)
    full_copy.start()
    own_weights = w_ref[pl.ds(z * 2 + xl, 1), :]
    full_copy.wait()

    coeffs = full[0:ROWS, :]
    scaled = coeffs * own_weights
    contract = (((1,), (1,)), ((), ()))
    upper = lax.dot_general(
        scaled, full[0:LANES, :], contract,
        precision=lax.Precision.HIGHEST, preferred_element_type=F32,
    )
    corner = lax.dot_general(
        scaled[LANES:ROWS], full[LANES:256, :], contract,
        precision=lax.Precision.HIGHEST, preferred_element_type=F32,
    )
    terms[0:21] = upper.reshape(21, 8, LANES)
    terms[21:26] = corner.reshape(5, 8, LANES)

    plane_copies = []
    for dx, dy in PLANE[:-1]:
        j = len(plane_copies)
        xt, yt = lax.rem(x + dx, X), lax.rem(y + dy, Y)
        copy = remote(
            terms.at[(xt * Y + yt) * 2 + core], plane_in.at[j], plane_s.at[j], plane_r.at[j],
            place(xt, yt, z, core),
        )
        copy.start()
        plane_copies.append(copy)
    own = (x * Y + y) * 2 + core
    tile = terms[own]
    for j, copy in reversed(list(enumerate(plane_copies))):
        copy.wait_recv()
        tile = tile + plane_in[j]

    own_tile[...] = tile
    line_copies = []
    for j in (3, 2, 4, 1, 5, 0, 6):
        copy = remote(own_tile, line_in.at[j], line_s.at[j], line_r.at[j], line[j])
        copy.start()
        line_copies.append((j, copy))
    for j, copy in reversed(line_copies):
        copy.wait_recv()
        tile = tile + line_in[j]

    tiles[own] = tile
    all_copies = []
    for device, *_ in plane:
        j = len(all_copies)
        copy = remote(tiles.at[own], tiles.at[own], all_s.at[j], all_r.at[j], device)
        copy.start()
        all_copies.append(copy)
    for j, (_, dx, dy, flip) in enumerate(plane):
        xs, ys = lax.rem(x + X - dx, X), lax.rem(y + Y - dy, Y)
        cs = core if flip == 0 else other
        slot = tiles.at[(xs * Y + ys) * 2 + cs]
        remote(slot, slot, all_s.at[j], all_r.at[j], core_peer).wait_recv()
    for copy in core_copies + x_copies + z_copies + plane_copies + all_copies:
        copy.wait_send()
    for _, copy in line_copies:
        copy.wait_send()
    out_ref[...] = tiles[...]


def reduced_tiles(matching, vectors, weights):
    dma = pltpu.SemaphoreType.DMA
    depth = matching.shape[1]
    return pl.pallas_call(
        kernel,
        out_shape=jax.ShapeDtypeStruct((TILES, 8, LANES), F32),
        in_specs=[
            pl.BlockSpec(memory_space=pl.ANY),
            pl.BlockSpec(memory_space=pl.ANY),
            pl.BlockSpec(memory_space=pltpu.VMEM),
        ],
        out_specs=pl.BlockSpec(memory_space=pltpu.VMEM),
        scratch_shapes=[
            pltpu.VMEM((CH, depth), jnp.bfloat16),
            pltpu.VMEM((Z, depth, 256), jnp.bfloat16),
            pltpu.VMEM((Z, 2, ROWS, LANES), F32),
            pltpu.VMEM((Z, 2, HALF, LANES), F32),
            pltpu.VMEM((Z, 2, HALF, LANES), F32),
            pltpu.VMEM((Z, HALF, LANES), F32),
            pltpu.VMEM((Z, HALF, LANES), F32),
            pltpu.VMEM((Z - 1, HALF, LANES), F32),
            pltpu.VMEM((256, LANES), F32),
            pltpu.VMEM((TILES, 8, LANES), F32),
            pltpu.VMEM((15, 8, LANES), F32),
            pltpu.VMEM((8, LANES), F32),
            pltpu.VMEM((7, 8, LANES), F32),
            pltpu.VMEM((TILES, 8, LANES), F32),
            dma, dma((Z,)),
            dma((Z,)), dma((Z,)), dma((Z,)), dma((Z,)), dma((Z - 1,)), dma((Z - 1,)), dma, dma,
            dma((15,)), dma((15,)), dma((7,)), dma((7,)), dma((31,)), dma((31,)),
        ],
        compiler_params=pltpu.CompilerParams(
            collective_id=0, has_side_effects=True, vmem_limit_bytes=40 * 1024 * 1024
        ),
        name="reduced_tiles",
    )(matching, vectors, weights.reshape(-1, LANES))


def gaunt_density(density_matrix, gaunt_index, gaunt_value):
    harmonics = density_matrix.shape[0] // 2
    codes = jnp.arange(harmonics, dtype=jnp.int32)[:, None]
    first_table = (gaunt_index[0][None, :] == codes).astype(F32)
    second_table = (gaunt_index[1][None, :] == codes).astype(F32)
    target_table = (gaunt_index[2][None, :] == codes).astype(F32)
    collected = []
    for radial in range(2):
        for other in range(2):
            block = density_matrix[
                radial * harmonics : (radial + 1) * harmonics,
                other * harmonics : (other + 1) * harmonics,
            ]
            spread = jnp.dot(
                block, second_table, precision=lax.Precision.HIGHEST, preferred_element_type=F32
            )
            collected.append(jnp.sum(spread * first_table, axis=0) * gaunt_value)
    return lax.dot_general(
        jnp.stack(collected), target_table, (((1,), (1,)), ((), ())),
        precision=lax.Precision.HIGHEST, preferred_element_type=F32,
    )


def body(matching, vectors, weights, gaunt_index, gaunt_value):
    tiles = reduced_tiles(matching, vectors, weights)
    left = tiles[:21].reshape(ROWS, LANES)[:CH]
    corner = tiles[21:26].reshape(40, LANES)[: CH - LANES, : CH - LANES]
    right = jnp.concatenate([left[LANES:].T, corner], axis=0)
    density_matrix = jnp.concatenate([left, right], axis=1)
    return density_matrix, gaunt_density(density_matrix, gaunt_index, gaunt_value)


def solution(mesh):
    return jax.shard_map(
        body,
        mesh=mesh,
        in_specs=(P(None, "basis"), P("basis", "band"), P("band"), P(), P()),
        out_specs=(P(), P()),
        check_vma=False,
    )
```

time: 121 us -> 57.6 us (0.48)
  Pallas kernels: 0 us -> 44.8 us
  blocking collectives: 43.3 us -> 0 us
  waiting for transfers between devices: 33.7 us -> 0 us
  local copies, waits for them, and re-layouts: 17.4 us -> 6.11 us
  starting transfers between devices: 10.1 us -> 0 us
  matrix products: 13.6 us -> 5.08 us
    pallas_call x0 -> x1, Pallas kernels: none -> 44.8 us  [reduced_tiles(): pl.pallas_call(kernel, out_shape=jax.ShapeDtypeStruct((TILES, 8, LANES),...]
    all_to_all x3 -> x0, blocking collectives: 43.3 us -> none  [the longest x1 27.2 us: sum_by_axis(): lax.all_to_all(nearer, far, split_axis=0, concat_axis=0, tiled=True)]
    all_to_all x2 -> x0, waiting for transfers between devices: 33.7 us -> none  [sent_to_all(): return lax.all_to_all(copies, axis, split_axis=0, concat_axis=0, tiled=True)]
    all_to_all x2 -> x0, starting transfers between devices: 10.1 us -> none  [sent_to_all(): return lax.all_to_all(copies, axis, split_axis=0, concat_axis=0, tiled=True)]
    dot_general x3 -> x1, matrix products: 9.94 us -> 1.39 us  [gaunt_density(): lax.dot_general(jnp.stack(collected), target_table, (((1,), (1,)), ((), (...]
    another operation x3 -> x0, local copies, waits for them, and re-layouts: 7.11 us -> none  [the longest x1 3.6 us: total_of(): return whole[:len(lines)].reshape(shard.shape)]
    unnamed x15 -> x11, local copies, waits for them, and re-layouts: 1.23 us -> 5.95 us
    mul x3 -> x0, local copies, waits for them, and re-layouts: 4.38 us -> none  [weighted_pairs(): scaled = coeffs * band_weights[None, :]]
  transfers between devices with their start and end apart: 2 -> 0, of which waited for: 2 -> 0; matrix products, arithmetic and copies ran while one was open for 2% -> 0% of each run, Pallas kernels for 0% -> 0%
where the time goes in v1:
time: 57.6 us; the launch traced here: 57.4 us
  Pallas kernels  44.8 us (78%)
  local copies, waits for them, and re-layouts  6.11 us (11%)
  matrix products  5.08 us (9%)
  between operations  0.74 us (1%)
  other arithmetic  0.71 us (1%)
    pallas_call x1, Pallas kernels, reduced_tiles(): pl.pallas_call(kernel, out_shape=jax.ShapeDtypeStruct((TILES, 8, LANES),...  44.8 us
    unnamed x11, local copies, waits for them, and re-layouts  5.95 us
    dot_general x4, matrix products, gaunt_density(): jnp.dot(block, second_table, precision=lax.Precision.HIGHEST, preferred_e...  3.69 us
    dot_general x1, matrix products, gaunt_density(): lax.dot_general(jnp.stack(collected), target_table, (((1,), (1,)), ((), (...  1.39 us

profile of v1, /device:TPU:1, one launch (start us, length us, event | category | flops | bytes accessed | tf_op | source)
XLA Modules:
  0.0 57.4 jit_solution(16782689614527454824)
XLA Ops:
  0.6 0.0 copy-start
  0.6 4.0 %copy-done = bf16[2560,2048]{1,0:T(8,128)(2,1)S(1)} copy-done((bf16[2560,2048]{1,0:T(8,128)(2,1)S(1)}, bf16[2560,2048]{1,0:T(8,128)(2,1)}, u32[]{:S(2)}) %copy-start) | copy-done | bytes 10485784
  4.6 0.0 copy-start.1
  4.6 1.2 %copy-done.1 = bf16[162,2560]{1,0:T(8,128)(2,1)S(1)} copy-done((bf16[162,2560]{1,0:T(8,128)(2,1)S(1)}, bf16[162,2560]{1,0:T(8,128)(2,1)}, u32[]{:S(2)}) %copy-start.1) | copy-done | bytes 829464
  5.8 0.0 copy-start.2
  5.8 0.7 %copy-done.2 = f32[2048]{0:T(1024)S(1)} copy-done((f32[2048]{0:T(1024)S(1)}, f32[2048]{0:T(1024)}, u32[]{:S(2)}) %copy-start.2) | copy-done | bytes 8216
  6.5 0.0 copy-start.3
  6.5 44.8 %reduced_tiles.1 = f32[32,8,128]{2,1,0:T(8,128)S(1)} custom-call(bf16[162,2560]{1,0:T(8,128)(2,1)S(1)} %copy-done.1, bf16[2560,2048]{1,0:T(8,128)(2,1)S(1)} %copy-done, f32[16,128]{1,0:T(8,128)S(1)} %bitcast.16), custom_call_target="tpu_custom_call" | custom-call | tf_op jit(solution)/shard_map/reduced_tiles/pallas_call | solution.py:199
  51.3 0.1 copy.10
  51.4 0.1 copy.9
  51.5 0.0 copy-done.3
  51.6 0.9 %fusion.4 = f32[4096]{0:T(1024)S(1)} fusion(s32[4096]{0:T(1024)S(1)} %bitcast.30, s32[4096]{0:T(1024)S(1)} %bitcast.26, f32[162,128]{1,0:T(8,128)S(1)} %bitcast.17, f32[162,34]{1,0:T(8,128)S(1)} %copy.9), kind=kOutput, calls=%fused_computation.11 | convolution fusion | flops 323815840 | bytes 154128 | tf_op jit(solution)/shard_map/dot_general | solution.py:247
  52.5 0.9 %fusion.2 = f32[4096]{0:T(1024)S(1)} fusion(s32[4096]{0:T(1024)S(1)} %bitcast.31, s32[4096]{0:T(1024)S(1)} %bitcast.27, f32[162,128]{1,0:T(8,128)S(1)} %bitcast.18, f32[162,34]{1,0:T(8,128)S(1)} %copy.9), kind=kOutput, calls=%fused_computation.9 | convolution fusion | flops 323815840 | bytes 154128 | tf_op jit(solution)/shard_map/dot_general | solution.py:247
  53.5 0.0 copy-start.4
  53.5 0.9 %fusion.1 = f32[4096]{0:T(1024)S(1)} fusion(s32[4096]{0:T(1024)S(1)} %bitcast.32, s32[4096]{0:T(1024)S(1)} %bitcast.28, f32[168,128]{1,0:T(8,128)S(1)} %slice_bitcast_fusion), kind=kOutput, calls=%fused_computation.8 | convolution fusion | flops 323809280 | bytes 94208 | tf_op jit(solution)/shard_map/dot_general | solution.py:247
  54.4 0.9 %fusion.3 = f32[4096]{0:T(1024)S(1)} fusion(s32[4096]{0:T(1024)S(1)} %bitcast.33, s32[4096]{0:T(1024)S(1)} %bitcast.29, f32[168,128]{1,0:T(8,128)S(1)} %slice_bitcast_fusion), kind=kOutput, calls=%fused_computation.10 | convolution fusion | flops 323809280 | bytes 94208 | tf_op jit(solution)/shard_map/dot_general | solution.py:247
  55.3 0.0 copy-done.4
  55.3 1.4 %fusion = f32[4,81]{1,0:T(4,128)} fusion(s32[4096]{0:T(1024)S(1)} %bitcast.25, f32[1,4096]{1,0:T(1,128)S(1)} %bitcast.23, f32[1,4096]{1,0:T(1,128)S(1)} %bitcast.24, f32[1,4096]{1,0:T(1,128)S(1)} %bitcast.22, f32[1,4096]{1,0:T(1,128)S(1)} %bitcast.21), kind=kOutput, calls=%fused_computation.7 | convolution fusion | flops 16306176 | bytes 83216 | tf_op jit(solution)/shard_map/dot_general | solution.py:251
  56.7 0.7 %pad_maximum_fusion = f32[162,162]{1,0:T(8,128)} fusion(f32[162,34]{1,0:T(8,128)S(1)} %copy.9, f32[162,128]{1,0:T(8,128)S(1)} %bitcast.19), kind=kLoop, calls=%fused_computation.19 | loop fusion | flops 26244 | bytes 209952 | tf_op jit(solution)/shard_map/concatenate | solution.py:262
  (6 shorter events, 0.1 us)
Async XLA Ops:
  0.6 4.0 %copy-start = (bf16[2560,2048]{1,0:T(8,128)(2,1)S(1)}, bf16[2560,2048]{1,0:T(8,128)(2,1)}, u32[]{:S(2)}) copy-start(bf16[2560,2048]{1,0:T(8,128)(2,1)} %v_hbm.1) | copy-start | bytes 31457284
  4.6 1.2 %copy-start.1 = (bf16[162,2560]{1,0:T(8,128)(2,1)S(1)}, bf16[162,2560]{1,0:T(8,128)(2,1)}, u32[]{:S(2)}) copy-start(bf16[162,2560]{1,0:T(8,128)(2,1)} %a_hbm.1) | copy-start | bytes 2488324
  5.8 0.7 %copy-start.2 = (f32[2048]{0:T(1024)S(1)}, f32[2048]{0:T(1024)}, u32[]{:S(2)}) copy-start(f32[2048]{0:T(1024)} %param.7) | copy-start | bytes 24580
  6.5 45.1 %copy-start.3 = (s32[3,4096]{1,0:T(4,128)S(1)}, s32[3,4096]{1,0:T(4,128)}, u32[]{:S(2)}) copy-start(s32[3,4096]{1,0:T(4,128)} %param.8) | copy-start | bytes 147460
  53.5 1.9 %copy-start.4 = (f32[4096]{0:T(1024)S(1)}, f32[4096]{0:T(1024)}, u32[]{:S(2)}) copy-start(f32[4096]{0:T(1024)} %param.9) | copy-start | bytes 49156

commit v2 on v1

v2 whole, which is shorter than its diff:
```python
import jax
import jax.numpy as jnp
from jax import lax
from jax.experimental import pallas as pl
from jax.experimental.pallas import tpu as pltpu
from jax.sharding import PartitionSpec as P

CH = 162
ROWS = 168
HALF = 88
SHIFT = 80
Z = 8
X = 4
Y = 4
LANES = 128
TILES = 32
HARM = 81
ENTRIES = 4096
CHUNK = 512
OFFSETS = (4, 3, 5, 2, 6, 1, 7, 0)
PLANE = tuple((dx, dy) for dx in (2, 1, 3, 0) for dy in (2, 1, 3, 0))
MESH = pl.DeviceIdType.MESH
F32 = jnp.float32
BF16 = jnp.bfloat16


def place(x, y, z, core):
    return {
        "basis": (z * 2 + lax.rem(x, 2)) * 2 + core,
        "band": lax.div(x, 2) * Y + y,
    }


def halves(value):
    high = value.astype(BF16)
    return high, (value - high.astype(F32)).astype(BF16)


def harmonic_of(channel):
    folded = jnp.where(channel >= HARM, channel - HARM, channel)
    return jnp.where(channel < CH, folded, -1)


def kernel(
    a_hbm, v_hbm, w_hbm, index_hbm, value_hbm, matrix_ref, density_ref,
    a_buf, v_buf, part, core_in, pair, x_in, z_out, z_in, full, terms, plane_in,
    own_tile, line_in, tiles, w_buf, index_buf, value_buf, hot, target_hot, factor, sums,
    a_sem, v_sem, table_sem, core_s, core_r, x_s, x_r, z_s, z_r, full_s, full_r,
    plane_s, plane_r, line_s, line_r, all_s, all_r, sum_s, sum_r,
):
    basis, band = lax.axis_index("basis"), lax.axis_index("band")
    z, xl, core = lax.div(basis, 4), lax.rem(lax.div(basis, 2), 2), lax.rem(basis, 2)
    x, y = lax.div(band, Y) * 2 + xl, lax.rem(band, Y)
    other = 1 - core
    own = (x * Y + y) * 2 + core

    a_copy = pltpu.make_async_copy(a_hbm, a_buf, a_sem)
    a_copy.start()
    targets = [lax.rem(z + off, Z) for off in OFFSETS]
    v_copies = []
    for s in range(Z):
        columns = pl.ds(pl.multiple_of(targets[s] * 256, 256), 256)
        place_in = v_buf.at[s // 2, :, (s % 2) * 256 : (s % 2) * 256 + 256]
        v_copies.append(pltpu.make_async_copy(v_hbm.at[:, columns], place_in, v_sem.at[s]))
    for s in range(4):
        v_copies[s].start()
    table_copies = [
        pltpu.make_async_copy(w_hbm, w_buf, table_sem.at[0]),
        pltpu.make_async_copy(index_hbm, index_buf, table_sem.at[1]),
        pltpu.make_async_copy(value_hbm, value_buf, table_sem.at[2]),
    ]

    plane = [
        (place(lax.rem(x + dx, X), lax.rem(y + dy, Y), z, c), dx, dy, flip)
        for dx, dy in PLANE
        for flip, c in ((0, core), (1, other))
        if (dx, dy, flip) != (0, 0, 0)
    ]
    line = [place(x, y, lax.rem(z + dz, Z), core) for dz in range(1, Z)]
    barrier = pltpu.get_barrier_semaphore()
    for device, *_ in plane:
        pl.semaphore_signal(barrier, inc=1, device_id=device, device_id_type=MESH)
    for device in line:
        pl.semaphore_signal(barrier, inc=1, device_id=device, device_id_type=MESH)

    for s in range(Z):
        for h in range(2):
            part[s, h, SHIFT * 2 : ROWS, :] = jnp.zeros((ROWS - SHIFT * 2, LANES), F32)
    full[ROWS:256, :] = jnp.zeros((256 - ROWS, LANES), F32)
    terms[26:TILES] = jnp.zeros((TILES - 26, 8, LANES), F32)

    core_peer = place(x, y, z, other)
    x_peer = place(x + 1 - 2 * xl, y, z, core)

    def remote(src, dst, send, recv, device):
        return pltpu.make_async_remote_copy(
            src_ref=src, dst_ref=dst, send_sem=send, recv_sem=recv,
            device_id=device, device_id_type=MESH,
        )

    mine = pl.ds(pl.multiple_of(SHIFT * core, 8), HALF)
    theirs = pl.ds(pl.multiple_of(SHIFT * other, 8), HALF)
    core_copies, x_copies, z_copies = [], [], []
    plane_copies, line_copies, all_copies = [], [], []

    def multiply(c):
        v_copies[2 * c].wait()
        v_copies[2 * c + 1].wait()
        if c + 2 < Z // 2:
            v_copies[2 * c + 4].start()
            v_copies[2 * c + 5].start()
        product = jnp.dot(a_buf[...], v_buf[c], preferred_element_type=F32)
        for s in (2 * c, 2 * c + 1):
            for h in range(2):
                at = (s % 2) * 256 + h * LANES
                part[s, h, 0:CH, :] = product[:, at : at + LANES]

    def to_core(s):
        copy = remote(part.at[s, :, theirs, :], core_in.at[s], core_s.at[s], core_r.at[s], core_peer)
        copy.start()
        core_copies.append(copy)

    def to_x(s):
        core_copies[s].wait_recv()
        pair[s] = part[s, :, mine, :] + core_in[s]
        copy = remote(pair.at[s, 1 - xl], x_in.at[s], x_s.at[s], x_r.at[s], x_peer)
        copy.start()
        x_copies.append(copy)

    def to_z(s):
        x_copies[s].wait_recv()
        z_out[s] = pair[s, xl] + x_in[s]
        if OFFSETS[s]:
            copy = remote(
                z_out.at[s], z_in.at[s], z_s.at[s], z_r.at[s], place(x, y, targets[s], core)
            )
            copy.start()
            z_copies.append(copy)

    first_row = own * 8 - jnp.where(own < 21, 0, 40)
    first_column = jnp.where(own < 21, 0, LANES)
    mirrored = jnp.where(jnp.logical_and(own >= 16, own < 21), 1.0, 0.0).astype(F32)
    row_channel = first_row + lax.broadcasted_iota(jnp.int32, (8, 1), 0)

    def tables(n):
        at = slice(n * CHUNK, (n + 1) * CHUNK)
        first, second = index_buf[0:1, at], index_buf[1:2, at]
        target, value = index_buf[2:3, at], value_buf[0:1, at]
        column = harmonic_of(first_column + lax.broadcasted_iota(jnp.int32, (LANES, 1), 0))
        hot[0:LANES, at] = jnp.where(column == second, 1.0, 0.0).astype(BF16)
        hot[LANES : 2 * LANES, at] = jnp.where(column == first, 1.0, 0.0).astype(BF16)
        code = lax.broadcasted_iota(jnp.int32, (LANES, 1), 0)
        target_hot[:, at] = jnp.where(code == target, 1.0, 0.0).astype(BF16)
        row = harmonic_of(row_channel)
        factor[0:8, at] = jnp.where(row == first, value, 0.0)
        factor[8:16, at] = jnp.where(row == second, value, 0.0) * mirrored

    def contracted(tile):
        lane = first_column + lax.broadcasted_iota(jnp.int32, (8, LANES), 1)
        none = jnp.zeros((8, LANES), F32)
        lows = jnp.where(lane < HARM, tile, 0.0)
        highs = jnp.where(lane < HARM, 0.0, tile)
        wide = jnp.concatenate(
            [
                jnp.concatenate([lows, highs, none, none], axis=0),
                jnp.concatenate([none, none, lows, highs], axis=0),
            ],
            axis=1,
        )
        both = jnp.concatenate(halves(wide), axis=0)
        total = jnp.zeros((8, LANES), F32)
        for n in range(ENTRIES // 1024):
            at = slice(n * 1024, (n + 1) * 1024)
            spread = jnp.dot(both, hot[:, at], preferred_element_type=F32)
            spread = spread[0:32] + spread[32:64]
            direct, mirror = factor[0:8, at], factor[8:16, at]
            low, high = spread[0:8] * direct, spread[8:16] * direct
            mirror_low, mirror_high = spread[16:24] * mirror, spread[24:32] * mirror
            upper = row_channel >= HARM
            rows = [
                jnp.where(upper, 0.0, low),
                jnp.where(upper, 0.0, high) + mirror_low,
                jnp.where(upper, low, 0.0),
                jnp.where(upper, high, 0.0) + mirror_high,
            ]
            values = jnp.concatenate([jnp.sum(row, axis=0, keepdims=True) for row in rows], axis=0)
            total = total + lax.dot_general(
                jnp.concatenate(halves(values), axis=0), target_hot[:, at],
                (((1,), (1,)), ((), ())), preferred_element_type=F32,
            )
        return total[0:4] + total[4:8]

    def finish():
        for copy in core_copies + x_copies + z_copies + plane_copies + line_copies + all_copies:
            copy.wait_send()

    a_copy.wait()
    multiply(0)
    pl.semaphore_wait(barrier, len(plane) + len(line))
    to_core(0)
    to_core(1)
    for copy in table_copies:
        copy.start()
    multiply(1)
    to_core(2)
    to_core(3)
    to_x(0)
    to_x(1)
    multiply(2)
    to_core(4)
    to_core(5)
    to_x(2)
    to_x(3)
    multiply(3)
    to_core(6)
    to_core(7)
    to_x(4)
    to_x(5)
    for copy in table_copies:
        copy.wait()
    to_x(6)
    to_x(7)
    for s in range(Z):
        tables(s)
        to_z(s)
    total = z_out[Z - 1]
    for s in range(Z - 1):
        z_copies[s].wait_recv()
        total = total + z_in[s]

    full[mine, :] = total
    sent = pl.ds(pl.multiple_of(HALF * core, 8), SHIFT)
    full_copy = remote(full.at[sent, :], full.at[sent, :], full_s, full_r, core_peer)
    full_copy.start()
    own_weights = w_buf[pl.ds(z * 2 + xl, 1), :]
    full_copy.wait()

    coeffs = full[...]
    high, low = halves(coeffs)
    scaled_high, scaled_low = halves(coeffs[0:ROWS] * own_weights)
    product = lax.dot_general(
        jnp.concatenate([scaled_high, scaled_low, scaled_high], axis=1),
        jnp.concatenate([high, high, low], axis=1),
        (((1,), (1,)), ((), ())), preferred_element_type=F32,
    )
    terms[0:21] = product[:, 0:LANES].reshape(21, 8, LANES)
    terms[21:26] = product[LANES:ROWS, LANES:256].reshape(5, 8, LANES)

    for dx, dy in PLANE[:-1]:
        j = len(plane_copies)
        xt, yt = lax.rem(x + dx, X), lax.rem(y + dy, Y)
        copy = remote(
            terms.at[(xt * Y + yt) * 2 + core], plane_in.at[j], plane_s.at[j], plane_r.at[j],
            place(xt, yt, z, core),
        )
        copy.start()
        plane_copies.append(copy)
    tile = terms[own]
    for j, copy in reversed(list(enumerate(plane_copies))):
        copy.wait_recv()
        tile = tile + plane_in[j]

    own_tile[...] = tile
    for j in (3, 2, 4, 1, 5, 0, 6):
        copy = remote(own_tile, line_in.at[j], line_s.at[j], line_r.at[j], line[j])
        copy.start()
        line_copies.append(copy)
    for j, copy in reversed(list(zip((3, 2, 4, 1, 5, 0, 6), line_copies))):
        copy.wait_recv()
        tile = tile + line_in[j]

    def to_all(buffer, send, recv):
        for j, (device, *_) in enumerate(plane):
            copy = remote(buffer.at[own], buffer.at[own], send.at[j], recv.at[j], device)
            copy.start()
            all_copies.append(copy)

    def from_all(buffer, send, recv):
        for j, (_, dx, dy, flip) in enumerate(plane):
            xs, ys = lax.rem(x + X - dx, X), lax.rem(y + Y - dy, Y)
            slot = buffer.at[(xs * Y + ys) * 2 + (core if flip == 0 else other)]
            remote(slot, slot, send.at[j], recv.at[j], core_peer).wait_recv()

    tiles[own] = tile
    to_all(tiles, all_s, all_r)
    sums[own] = contracted(tile)
    to_all(sums, sum_s, sum_r)
    from_all(tiles, all_s, all_r)
    left = tiles[0:21].reshape(ROWS, LANES)
    matrix_ref[:, 0:LANES] = left[0:CH]
    matrix_ref[0:LANES, LANES:CH] = left[LANES:ROWS].T[:, 0 : CH - LANES]
    matrix_ref[LANES:CH, LANES:CH] = tiles[21:26].reshape(40, LANES)[0 : CH - LANES, 0 : CH - LANES]
    from_all(sums, sum_s, sum_r)
    density_ref[...] = jnp.sum(sums[...], axis=0)[:, 0:HARM]
    finish()


def body(matching, vectors, weights, gaunt_index, gaunt_value):
    dma = pltpu.SemaphoreType.DMA
    depth = matching.shape[1]
    return pl.pallas_call(
        kernel,
        out_shape=(
            jax.ShapeDtypeStruct((CH, CH), F32),
            jax.ShapeDtypeStruct((4, HARM), F32),
        ),
        in_specs=[pl.BlockSpec(memory_space=pl.ANY)] * 5,
        out_specs=(
            pl.BlockSpec(memory_space=pltpu.VMEM),
            pl.BlockSpec(memory_space=pltpu.VMEM),
        ),
        scratch_shapes=[
            pltpu.VMEM((CH, depth), BF16),
            pltpu.VMEM((Z // 2, depth, 512), BF16),
            pltpu.VMEM((Z, 2, ROWS, LANES), F32),
            pltpu.VMEM((Z, 2, HALF, LANES), F32),
            pltpu.VMEM((Z, 2, HALF, LANES), F32),
            pltpu.VMEM((Z, HALF, LANES), F32),
            pltpu.VMEM((Z, HALF, LANES), F32),
            pltpu.VMEM((Z - 1, HALF, LANES), F32),
            pltpu.VMEM((256, LANES), F32),
            pltpu.VMEM((TILES, 8, LANES), F32),
            pltpu.VMEM((15, 8, LANES), F32),
            pltpu.VMEM((8, LANES), F32),
            pltpu.VMEM((7, 8, LANES), F32),
            pltpu.VMEM((TILES, 8, LANES), F32),
            pltpu.VMEM((16, LANES), F32),
            pltpu.VMEM((3, ENTRIES), jnp.int32),
            pltpu.VMEM((1, ENTRIES), F32),
            pltpu.VMEM((2 * LANES, ENTRIES), BF16),
            pltpu.VMEM((LANES, ENTRIES), BF16),
            pltpu.VMEM((16, ENTRIES), F32),
            pltpu.VMEM((TILES, 4, LANES), F32),
            dma, dma((Z,)), dma((3,)),
            dma((Z,)), dma((Z,)), dma((Z,)), dma((Z,)), dma((Z - 1,)), dma((Z - 1,)), dma, dma,
            dma((15,)), dma((15,)), dma((7,)), dma((7,)),
            dma((31,)), dma((31,)), dma((31,)), dma((31,)),
        ],
        compiler_params=pltpu.CompilerParams(
            collective_id=0, has_side_effects=True, vmem_limit_bytes=67_043_328
        ),
        name="muffin_tin",
    )(matching, vectors, weights.reshape(-1, LANES), gaunt_index, gaunt_value.reshape(1, -1))


def solution(mesh):
    return jax.shard_map(
        body,
        mesh=mesh,
        in_specs=(P(None, "basis"), P("basis", "band"), P("band"), P(), P()),
        out_specs=(P(), P()),
        check_vma=False,
    )
```

time: 57.6 us -> 48.3 us (0.84)
  matrix products: 5.08 us -> 0 us
  local copies, waits for them, and re-layouts: 6.11 us -> 2.84 us
  other arithmetic: 0.71 us -> 0 us
    dot_general x5 -> x0, matrix products: 5.08 us -> none  [the longest x4 3.69 us: gaunt_density(): jnp.dot(block, second_table, precision=lax.Precision.HIGHEST, preferred_e...]
    unnamed x11 -> x2, local copies, waits for them, and re-layouts: 5.95 us -> 2.84 us
    concatenate x2 -> x0, other arithmetic: 0.7 us -> none  [the longest x1 0.69 us: body(): density_matrix = jnp.concatenate([left, right], axis=1)]
where the time goes in v2:
time: 48.3 us; the launch traced here: 48.1 us
  Pallas kernels  44.7 us (93%)
  local copies, waits for them, and re-layouts  2.84 us (6%)
  between operations  0.64 us (1%)
    pallas_call x1, Pallas kernels, body(): pl.pallas_call(kernel, out_shape=(jax.ShapeDtypeStruct((CH, CH), F32), ja...  44.7 us
    unnamed x2, local copies, waits for them, and re-layouts  2.84 us

profile of v2, /device:TPU:1, one launch (start us, length us, event | category | flops | bytes accessed | tf_op | source)
XLA Modules:
  0.0 48.1 jit_solution(9119856549797386193)
XLA Ops:
  0.6 44.7 %muffin_tin.1 = (f32[162,162]{1,0:T(8,128)}, f32[4,81]{1,0:T(4,128)}) custom-call(bf16[162,2560]{1,0:T(8,128)(2,1)} %a_hbm.1, bf16[2560,2048]{1,0:T(8,128)(2,1)} %v_hbm.1, f32[16,128]{1,0:T(8,128)} %bitcast.3, s32[3,4096]{1,0:T(4,128)} %index_hbm.1, f32[1,4096]{1,0:T(1,128)} %bitcast.2), custom_call_target="tpu_custom_call" | custom-call | tf_op jit(solution)/shard_map/muffin_tin/pallas_call | solution.py:301
  45.3 1.6 %copy.9 = f32[162,162]{1,0:T(8,128)} copy(f32[162,162]{1,0:T(8,128)} %get-tuple-element.4) | data formatting | bytes 209952
  46.9 1.2 %copy.10 = f32[4,81]{1,0:T(4,128)} copy(f32[4,81]{1,0:T(4,128)} %get-tuple-element.5) | data formatting | bytes 2592

commit v3 on v2

--- a/solution.py
+++ b/solution.py
@@ -17,7 +17,8 @@
 HARM = 81
 ENTRIES = 4096
 CHUNK = 512
-OFFSETS = (4, 3, 5, 2, 6, 1, 7, 0)
+GROUPS = ((4,), (3, 5), (1, 7), (2, 6), (0,))
+VIA = 48
 PLANE = tuple((dx, dy) for dx in (2, 1, 3, 0) for dy in (2, 1, 3, 0))
 MESH = pl.DeviceIdType.MESH
 F32 = jnp.float32
@@ -43,7 +44,8 @@
 
 def kernel(
     a_hbm, v_hbm, w_hbm, index_hbm, value_hbm, matrix_ref, density_ref,
-    a_buf, v_buf, part, core_in, pair, x_in, z_out, z_in, full, terms, plane_in,
+    a_buf, v_wide, v_slim, part, core_in, pair, x_in, z_out, far, thirds, nexts, seconds,
+    full, terms, plane_in,
     own_tile, line_in, tiles, w_buf, index_buf, value_buf, hot, target_hot, factor, sums,
     a_sem, v_sem, table_sem, core_s, core_r, x_s, x_r, z_s, z_r, full_s, full_r,
     plane_s, plane_r, line_s, line_r, all_s, all_r, sum_s, sum_r,
@@ -56,14 +58,21 @@
 
     a_copy = pltpu.make_async_copy(a_hbm, a_buf, a_sem)
     a_copy.start()
-    targets = [lax.rem(z + off, Z) for off in OFFSETS]
+    targets = [lax.rem(z + off, Z) for off in range(Z)]
+    v_blocks = (v_slim.at[0], v_wide.at[0], v_wide.at[1], v_wide.at[2], v_slim.at[1])
     v_copies = []
-    for s in range(Z):
-        columns = pl.ds(pl.multiple_of(targets[s] * 256, 256), 256)
-        place_in = v_buf.at[s // 2, :, (s % 2) * 256 : (s % 2) * 256 + 256]
-        v_copies.append(pltpu.make_async_copy(v_hbm.at[:, columns], place_in, v_sem.at[s]))
-    for s in range(4):
-        v_copies[s].start()
+    for group, block in zip(GROUPS, v_blocks):
+        copies = []
+        for h, off in enumerate(group):
+            columns = pl.ds(pl.multiple_of(targets[off] * 256, 256), 256)
+            copies.append(
+                pltpu.make_async_copy(
+                    v_hbm.at[:, columns], block.at[:, h * 256 : h * 256 + 256], v_sem.at[off]
+                )
+            )
+        v_copies.append(copies)
+    for copy in v_copies[0] + v_copies[1]:
+        copy.start()
     table_copies = [
         pltpu.make_async_copy(w_hbm, w_buf, table_sem.at[0]),
         pltpu.make_async_copy(index_hbm, index_buf, table_sem.at[1]),
@@ -100,42 +109,76 @@
 
     mine = pl.ds(pl.multiple_of(SHIFT * core, 8), HALF)
     theirs = pl.ds(pl.multiple_of(SHIFT * other, 8), HALF)
-    core_copies, x_copies, z_copies = [], [], []
+    core_copies, x_copies, z_copies = {}, {}, {}
     plane_copies, line_copies, all_copies = [], [], []
 
     def multiply(c):
-        v_copies[2 * c].wait()
-        v_copies[2 * c + 1].wait()
-        if c + 2 < Z // 2:
-            v_copies[2 * c + 4].start()
-            v_copies[2 * c + 5].start()
-        product = jnp.dot(a_buf[...], v_buf[c], preferred_element_type=F32)
-        for s in (2 * c, 2 * c + 1):
+        for copy in v_copies[c]:
+            copy.wait()
+        if c + 2 < len(GROUPS):
+            for copy in v_copies[c + 2]:
+                copy.start()
+        product = jnp.dot(a_buf[...], v_blocks[c][...], preferred_element_type=F32)
+        for g, off in enumerate(GROUPS[c]):
             for h in range(2):
-                at = (s % 2) * 256 + h * LANES
-                part[s, h, 0:CH, :] = product[:, at : at + LANES]
-
-    def to_core(s):
-        copy = remote(part.at[s, :, theirs, :], core_in.at[s], core_s.at[s], core_r.at[s], core_peer)
-        copy.start()
-        core_copies.append(copy)
-
-    def to_x(s):
-        core_copies[s].wait_recv()
-        pair[s] = part[s, :, mine, :] + core_in[s]
-        copy = remote(pair.at[s, 1 - xl], x_in.at[s], x_s.at[s], x_r.at[s], x_peer)
-        copy.start()
-        x_copies.append(copy)
-
-    def to_z(s):
-        x_copies[s].wait_recv()
-        z_out[s] = pair[s, xl] + x_in[s]
-        if OFFSETS[s]:
-            copy = remote(
-                z_out.at[s], z_in.at[s], z_s.at[s], z_r.at[s], place(x, y, targets[s], core)
-            )
-            copy.start()
-            z_copies.append(copy)
+                at = g * 256 + h * LANES
+                part[off, h, 0:CH, :] = product[:, at : at + LANES]
+
+    def to_core(off):
+        core_copies[off] = remote(
+            part.at[off, :, theirs, :], core_in.at[off], core_s.at[off], core_r.at[off], core_peer
+        )
+        core_copies[off].start()
+
+    def of_core(off):
+        core_copies[off].wait_recv()
+        return part[off, :, mine, :] + core_in[off]
+
+    def to_x(off, value):
+        pair[off] = value
+        x_copies[off] = remote(
+            pair.at[off, 1 - xl], x_in.at[off], x_s.at[off], x_r.at[off], x_peer
+        )
+        x_copies[off].start()
+
+    def of_x(off):
+        x_copies[off].wait_recv()
+        return pair[off, xl] + x_in[off]
+
+    def to_z(key, src, dst, step):
+        z_copies[key] = remote(
+            src, dst, z_s.at[len(z_copies)], z_r.at[len(z_copies)], place(x, y, targets[step], core)
+        )
+        z_copies[key].start()
+
+    def to_far():
+        z_out[4] = of_x(4)
+        to_z("up4", z_out.at[4, 0:VIA], far.at[0:VIA], 2)
+        to_z("down4", z_out.at[4, VIA:HALF], far.at[VIA:HALF], 6)
+
+    def to_third(off):
+        z_out[off] = of_x(off)
+        to_z(off, z_out.at[off], thirds.at[off // 4], 1 if off == 3 else 7)
+
+    def to_next(off):
+        pair[off] = of_core(off)
+        to_z(off, pair.at[off], nexts.at[off // 4], off)
+
+    def to_second(off):
+        value = of_x(off)
+        if off == 2:
+            z_copies["up4"].wait_recv()
+            z_copies[3].wait_recv()
+            value = value + thirds[0]
+            z_out[off, 0:VIA] = value[0:VIA] + far[0:VIA]
+            z_out[off, VIA:HALF] = value[VIA:HALF]
+        else:
+            z_copies["down4"].wait_recv()
+            z_copies[5].wait_recv()
+            value = value + thirds[1]
+            z_out[off, 0:VIA] = value[0:VIA]
+            z_out[off, VIA:HALF] = value[VIA:HALF] + far[VIA:HALF]
+        to_z(off, z_out.at[off], seconds.at[off // 4], off)
 
     first_row = own * 8 - jnp.where(own < 21, 0, 40)
     first_column = jnp.where(own < 21, 0, LANES)
@@ -191,42 +234,55 @@
         return total[0:4] + total[4:8]
 
     def finish():
-        for copy in core_copies + x_copies + z_copies + plane_copies + line_copies + all_copies:
+        for copies in (core_copies, x_copies, z_copies):
+            for copy in copies.values():
+                copy.wait_send()
+        for copy in plane_copies + line_copies + all_copies:
             copy.wait_send()
 
     a_copy.wait()
     multiply(0)
     pl.semaphore_wait(barrier, len(plane) + len(line))
-    to_core(0)
-    to_core(1)
+    to_core(4)
     for copy in table_copies:
         copy.start()
     multiply(1)
+    to_core(3)
+    to_core(5)
+    to_x(4, of_core(4))
+    multiply(2)
+    to_core(1)
+    to_core(7)
+    to_x(3, of_core(3))
+    to_x(5, of_core(5))
+    multiply(3)
     to_core(2)
-    to_core(3)
-    to_x(0)
-    to_x(1)
-    multiply(2)
-    to_core(4)
-    to_core(5)
-    to_x(2)
-    to_x(3)
-    multiply(3)
     to_core(6)
-    to_core(7)
-    to_x(4)
-    to_x(5)
+    to_next(1)
+    to_next(7)
+    multiply(4)
+    to_core(0)
+    to_far()
+    to_x(2, of_core(2))
+    to_x(6, of_core(6))
+    to_third(3)
+    to_third(5)
+    own_sum = of_core(0)
     for copy in table_copies:
         copy.wait()
-    to_x(6)
-    to_x(7)
-    for s in range(Z):
-        tables(s)
-        to_z(s)
-    total = z_out[Z - 1]
-    for s in range(Z - 1):
-        z_copies[s].wait_recv()
-        total = total + z_in[s]
+    for n in range(2):
+        tables(n)
+    z_copies[1].wait_recv()
+    z_copies[7].wait_recv()
+    to_x(0, own_sum + nexts[0] + nexts[1])
+    to_second(2)
+    to_second(6)
+    for n in range(2, Z):
+        tables(n)
+    total = of_x(0)
+    z_copies[2].wait_recv()
+    z_copies[6].wait_recv()
+    total = total + seconds[0] + seconds[1]
 
     full[mine, :] = total
     sent = pl.ds(pl.multiple_of(HALF * core, 8), SHIFT)
@@ -301,8 +357,8 @@
     return pl.pallas_call(
         kernel,
         out_shape=(
-            jax.ShapeDtypeStruct((CH, CH), F32),
-            jax.ShapeDtypeStruct((4, HARM), F32),
+            pltpu.VMEM((CH, CH), F32),
+            pltpu.VMEM((4, HARM), F32),
         ),
         in_specs=[pl.BlockSpec(memory_space=pl.ANY)] * 5,
         out_specs=(
@@ -311,13 +367,17 @@
         ),
         scratch_shapes=[
             pltpu.VMEM((CH, depth), BF16),
-            pltpu.VMEM((Z // 2, depth, 512), BF16),
+            pltpu.VMEM((3, depth, 512), BF16),
+            pltpu.VMEM((2, depth, 256), BF16),
             pltpu.VMEM((Z, 2, ROWS, LANES), F32),
             pltpu.VMEM((Z, 2, HALF, LANES), F32),
             pltpu.VMEM((Z, 2, HALF, LANES), F32),
             pltpu.VMEM((Z, HALF, LANES), F32),
             pltpu.VMEM((Z, HALF, LANES), F32),
-            pltpu.VMEM((Z - 1, HALF, LANES), F32),
+            pltpu.VMEM((HALF, LANES), F32),
+            pltpu.VMEM((2, HALF, LANES), F32),
+            pltpu.VMEM((2, 2, HALF, LANES), F32),
+            pltpu.VMEM((2, HALF, LANES), F32),
             pltpu.VMEM((256, LANES), F32),
             pltpu.VMEM((TILES, 8, LANES), F32),
             pltpu.VMEM((15, 8, LANES), F32),
@@ -332,12 +392,12 @@
             pltpu.VMEM((16, ENTRIES), F32),
             pltpu.VMEM((TILES, 4, LANES), F32),
             dma, dma((Z,)), dma((3,)),
-            dma((Z,)), dma((Z,)), dma((Z,)), dma((Z,)), dma((Z - 1,)), dma((Z - 1,)), dma, dma,
+            dma((Z,)), dma((Z,)), dma((Z,)), dma((Z,)), dma((Z,)), dma((Z,)), dma, dma,
             dma((15,)), dma((15,)), dma((7,)), dma((7,)),
             dma((31,)), dma((31,)), dma((31,)), dma((31,)),
         ],
         compiler_params=pltpu.CompilerParams(
-            collective_id=0, has_side_effects=True, vmem_limit_bytes=67_043_328
+            collective_id=0, has_side_effects=True, vmem_limit_bytes=66_500_000
         ),
         name="muffin_tin",
     )(matching, vectors, weights.reshape(-1, LANES), gaunt_index, gaunt_value.reshape(1, -1))

time: 48.3 us -> 44.8 us (0.928)
  Pallas kernels: 44.7 us -> 42.8 us
  local copies, waits for them, and re-layouts: 2.84 us -> 1.25 us
    pallas_call x1, Pallas kernels: 44.7 us -> 42.8 us  [body(): pl.pallas_call(kernel, out_shape=(pltpu.VMEM((CH, CH), F32), pltpu.VMEM((...]
    unnamed x2, local copies, waits for them, and re-layouts: 2.84 us -> 1.25 us
where the time goes in v3:
time: 44.8 us; the launch traced here: 44.7 us
  Pallas kernels  42.8 us (96%)
  local copies, waits for them, and re-layouts  1.25 us (3%)
  between operations  0.64 us (1%)
    pallas_call x1, Pallas kernels, body(): pl.pallas_call(kernel, out_shape=(pltpu.VMEM((CH, CH), F32), pltpu.VMEM((...  42.8 us
    unnamed x2, local copies, waits for them, and re-layouts  1.25 us

profile of v3, /device:TPU:1, one launch (start us, length us, event | category | flops | bytes accessed | tf_op | source)
XLA Modules:
  0.0 44.7 jit_solution(6929478531050463310)
XLA Ops:
  0.6 42.8 %muffin_tin.1 = (f32[162,162]{1,0:T(8,128)S(1)}, f32[4,81]{1,0:T(4,128)S(1)}) custom-call(bf16[162,2560]{1,0:T(8,128)(2,1)} %a_hbm.1, bf16[2560,2048]{1,0:T(8,128)(2,1)} %v_hbm.1, f32[16,128]{1,0:T(8,128)} %bitcast.3, s32[3,4096]{1,0:T(4,128)} %index_hbm.1, f32[1,4096]{1,0:T(1,128)} %bitcast.2), custom_call_target="tpu_custom_call" | custom-call | tf_op jit(solution)/shard_map/muffin_tin/pallas_call | solution.py:357
  43.5 0.7 %copy.9 = f32[162,162]{1,0:T(8,128)} copy(f32[162,162]{1,0:T(8,128)S(1)} %get-tuple-element.2) | data formatting | bytes 209952
  44.1 0.6 %copy.10 = f32[4,81]{1,0:T(4,128)} copy(f32[4,81]{1,0:T(4,128)S(1)} %get-tuple-element.3) | data formatting | bytes 2592

commit v4 on v3

--- a/solution.py
+++ b/solution.py
@@ -19,7 +19,10 @@
 CHUNK = 512
 GROUPS = ((4,), (3, 5), (1, 7), (2, 6), (0,))
 VIA = 48
-PLANE = tuple((dx, dy) for dx in (2, 1, 3, 0) for dy in (2, 1, 3, 0))
+PLANE = (
+    (2, 2), (2, 1), (2, 3), (1, 2), (3, 2), (2, 0), (0, 2), (1, 1),
+    (1, 3), (3, 1), (3, 3), (1, 0), (3, 0), (0, 1), (0, 3),
+)
 MESH = pl.DeviceIdType.MESH
 F32 = jnp.float32
 BF16 = jnp.bfloat16
@@ -46,15 +49,15 @@
     a_hbm, v_hbm, w_hbm, index_hbm, value_hbm, matrix_ref, density_ref,
     a_buf, v_wide, v_slim, part, core_in, pair, x_in, z_out, far, thirds, nexts, seconds,
     full, terms, plane_in,
-    own_tile, line_in, tiles, w_buf, index_buf, value_buf, hot, target_hot, factor, sums,
+    own_tile, line_in, tiles, w_buf, index_buf, value_buf, hot, target_hot, factor, sums, core_sums,
     a_sem, v_sem, table_sem, core_s, core_r, x_s, x_r, z_s, z_r, full_s, full_r,
-    plane_s, plane_r, line_s, line_r, all_s, all_r, sum_s, sum_r,
+    plane_s, plane_r, line_s, line_r, all_s, all_r, sum_s, sum_r, last_s, last_r,
 ):
     basis, band = lax.axis_index("basis"), lax.axis_index("band")
     z, xl, core = lax.div(basis, 4), lax.rem(lax.div(basis, 2), 2), lax.rem(basis, 2)
     x, y = lax.div(band, Y) * 2 + xl, lax.rem(band, Y)
     other = 1 - core
-    own = (x * Y + y) * 2 + core
+    own = core * 16 + x * Y + y
 
     a_copy = pltpu.make_async_copy(a_hbm, a_buf, a_sem)
     a_copy.start()
@@ -80,16 +83,13 @@
     ]
 
     plane = [
-        (place(lax.rem(x + dx, X), lax.rem(y + dy, Y), z, c), dx, dy, flip)
-        for dx, dy in PLANE
-        for flip, c in ((0, core), (1, other))
-        if (dx, dy, flip) != (0, 0, 0)
+        place(lax.rem(x + dx, X), lax.rem(y + dy, Y), z, core) for dx, dy in PLANE
     ]
+    core_peer = place(x, y, z, other)
     line = [place(x, y, lax.rem(z + dz, Z), core) for dz in range(1, Z)]
     barrier = pltpu.get_barrier_semaphore()
-    for device, *_ in plane:
-        pl.semaphore_signal(barrier, inc=1, device_id=device, device_id_type=MESH)
-    for device in line:
+    peers = plane + line + [core_peer]
+    for device in peers:
         pl.semaphore_signal(barrier, inc=1, device_id=device, device_id_type=MESH)
 
     for s in range(Z):
@@ -98,7 +98,6 @@
     full[ROWS:256, :] = jnp.zeros((256 - ROWS, LANES), F32)
     terms[26:TILES] = jnp.zeros((TILES - 26, 8, LANES), F32)
 
-    core_peer = place(x, y, z, other)
     x_peer = place(x + 1 - 2 * xl, y, z, core)
 
     def remote(src, dst, send, recv, device):
@@ -242,7 +241,7 @@
 
     a_copy.wait()
     multiply(0)
-    pl.semaphore_wait(barrier, len(plane) + len(line))
+    pl.semaphore_wait(barrier, len(peers))
     to_core(4)
     for copy in table_copies:
         copy.start()
@@ -302,13 +301,9 @@
     terms[0:21] = product[:, 0:LANES].reshape(21, 8, LANES)
     terms[21:26] = product[LANES:ROWS, LANES:256].reshape(5, 8, LANES)
 
-    for dx, dy in PLANE[:-1]:
-        j = len(plane_copies)
-        xt, yt = lax.rem(x + dx, X), lax.rem(y + dy, Y)
-        copy = remote(
-            terms.at[(xt * Y + yt) * 2 + core], plane_in.at[j], plane_s.at[j], plane_r.at[j],
-            place(xt, yt, z, core),
-        )
+    for j, (dx, dy) in enumerate(PLANE):
+        target = core * 16 + lax.rem(x + dx, X) * Y + lax.rem(y + dy, Y)
+        copy = remote(terms.at[target], plane_in.at[j], plane_s.at[j], plane_r.at[j], plane[j])
         copy.start()
         plane_copies.append(copy)
     tile = terms[own]
@@ -326,28 +321,39 @@
         tile = tile + line_in[j]
 
     def to_all(buffer, send, recv):
-        for j, (device, *_) in enumerate(plane):
-            copy = remote(buffer.at[own], buffer.at[own], send.at[j], recv.at[j], device)
-            copy.start()
-            all_copies.append(copy)
+        for j, device in enumerate(plane):
+            all_copies.append(remote(buffer.at[own], buffer.at[own], send.at[j], recv.at[j], device))
+            all_copies[-1].start()
 
     def from_all(buffer, send, recv):
-        for j, (_, dx, dy, flip) in enumerate(plane):
-            xs, ys = lax.rem(x + X - dx, X), lax.rem(y + Y - dy, Y)
-            slot = buffer.at[(xs * Y + ys) * 2 + (core if flip == 0 else other)]
+        for j, (dx, dy) in reversed(list(enumerate(PLANE))):
+            slot = buffer.at[
+                core * 16 + lax.rem(x + X - dx, X) * Y + lax.rem(y + Y - dy, Y)
+            ]
             remote(slot, slot, send.at[j], recv.at[j], core_peer).wait_recv()
+
+    def to_core_peer(ref, k):
+        all_copies.append(remote(ref, ref, last_s.at[k], last_r.at[k], core_peer))
+        all_copies[-1].start()
+        return all_copies[-1]
 
     tiles[own] = tile
     to_all(tiles, all_s, all_r)
     sums[own] = contracted(tile)
     to_all(sums, sum_s, sum_r)
     from_all(tiles, all_s, all_r)
+    own_half = pl.ds(pl.multiple_of(16 * core, 16), 16)
+    tiles_copy = to_core_peer(tiles.at[own_half], 0)
+    from_all(sums, sum_s, sum_r)
+    core_sums[core] = jnp.sum(sums[own_half], axis=0)
+    sums_copy = to_core_peer(core_sums.at[core], 1)
+    tiles_copy.wait_recv()
     left = tiles[0:21].reshape(ROWS, LANES)
     matrix_ref[:, 0:LANES] = left[0:CH]
     matrix_ref[0:LANES, LANES:CH] = left[LANES:ROWS].T[:, 0 : CH - LANES]
     matrix_ref[LANES:CH, LANES:CH] = tiles[21:26].reshape(40, LANES)[0 : CH - LANES, 0 : CH - LANES]
-    from_all(sums, sum_s, sum_r)
-    density_ref[...] = jnp.sum(sums[...], axis=0)[:, 0:HARM]
+    sums_copy.wait_recv()
+    density_ref[...] = (core_sums[0] + core_sums[1])[:, 0:HARM]
     finish()
 
 
@@ -391,10 +397,11 @@
             pltpu.VMEM((LANES, ENTRIES), BF16),
             pltpu.VMEM((16, ENTRIES), F32),
             pltpu.VMEM((TILES, 4, LANES), F32),
+            pltpu.VMEM((2, 4, LANES), F32),
             dma, dma((Z,)), dma((3,)),
             dma((Z,)), dma((Z,)), dma((Z,)), dma((Z,)), dma((Z,)), dma((Z,)), dma, dma,
             dma((15,)), dma((15,)), dma((7,)), dma((7,)),
-            dma((31,)), dma((31,)), dma((31,)), dma((31,)),
+            dma((15,)), dma((15,)), dma((15,)), dma((15,)), dma((2,)), dma((2,)),
         ],
         compiler_params=pltpu.CompilerParams(
             collective_id=0, has_side_effects=True, vmem_limit_bytes=66_500_000

time: 44.8 us -> 44.7 us (level)
  no operation moved by 1% of the time
where the time goes in v4:
time: 44.7 us; the launch traced here: 44.6 us
  Pallas kernels  42.7 us (96%)
  local copies, waits for them, and re-layouts  1.25 us (3%)
  between operations  0.64 us (1%)
    pallas_call x1, Pallas kernels, body(): pl.pallas_call(kernel, out_shape=(pltpu.VMEM((CH, CH), F32), pltpu.VMEM((...  42.7 us
    unnamed x2, local copies, waits for them, and re-layouts  1.25 us

profile of v4, /device:TPU:1, one launch (start us, length us, event | category | flops | bytes accessed | tf_op | source)
XLA Modules:
  0.0 44.6 jit_solution(18022582376130856600)
XLA Ops:
  0.6 42.7 %muffin_tin.1 = (f32[162,162]{1,0:T(8,128)S(1)}, f32[4,81]{1,0:T(4,128)S(1)}) custom-call(bf16[162,2560]{1,0:T(8,128)(2,1)} %a_hbm.1, bf16[2560,2048]{1,0:T(8,128)(2,1)} %v_hbm.1, f32[16,128]{1,0:T(8,128)} %bitcast.3, s32[3,4096]{1,0:T(4,128)} %index_hbm.1, f32[1,4096]{1,0:T(1,128)} %bitcast.2), custom_call_target="tpu_custom_call" | custom-call | tf_op jit(solution)/shard_map/muffin_tin/pallas_call | solution.py:363
  43.4 0.7 %copy.9 = f32[162,162]{1,0:T(8,128)} copy(f32[162,162]{1,0:T(8,128)S(1)} %get-tuple-element.2) | data formatting | bytes 209952
  44.0 0.6 %copy.10 = f32[4,81]{1,0:T(4,128)} copy(f32[4,81]{1,0:T(4,128)S(1)} %get-tuple-element.3) | data formatting | bytes 2592

commit v5 on v4

--- a/solution.py
+++ b/solution.py
@@ -74,7 +74,7 @@
                 )
             )
         v_copies.append(copies)
-    for copy in v_copies[0] + v_copies[1]:
+    for copy in v_copies[0] + v_copies[1] + v_copies[2]:
         copy.start()
     table_copies = [
         pltpu.make_async_copy(w_hbm, w_buf, table_sem.at[0]),
@@ -114,8 +114,8 @@
     def multiply(c):
         for copy in v_copies[c]:
             copy.wait()
-        if c + 2 < len(GROUPS):
-            for copy in v_copies[c + 2]:
+        if c + 3 < len(GROUPS):
+            for copy in v_copies[c + 3]:
                 copy.start()
         product = jnp.dot(a_buf[...], v_blocks[c][...], preferred_element_type=F32)
         for g, off in enumerate(GROUPS[c]):
@@ -252,8 +252,8 @@
     multiply(2)
     to_core(1)
     to_core(7)
+    to_x(5, of_core(5))
     to_x(3, of_core(3))
-    to_x(5, of_core(5))
     multiply(3)
     to_core(2)
     to_core(6)

time: 44.7 us -> 44.8 us (level)
  no operation moved by 1% of the time
where the time goes in v5:
time: 44.8 us; the launch traced here: 44.7 us
  Pallas kernels  42.8 us (96%)
  local copies, waits for them, and re-layouts  1.25 us (3%)
  between operations  0.64 us (1%)
    pallas_call x1, Pallas kernels, body(): pl.pallas_call(kernel, out_shape=(pltpu.VMEM((CH, CH), F32), pltpu.VMEM((...  42.8 us
    unnamed x2, local copies, waits for them, and re-layouts  1.25 us

profile of v5, /device:TPU:1, one launch (start us, length us, event | category | flops | bytes accessed | tf_op | source)
XLA Modules:
  0.0 44.7 jit_solution(15308553908161772246)
XLA Ops:
  0.6 42.8 %muffin_tin.1 = (f32[162,162]{1,0:T(8,128)S(1)}, f32[4,81]{1,0:T(4,128)S(1)}) custom-call(bf16[162,2560]{1,0:T(8,128)(2,1)} %a_hbm.1, bf16[2560,2048]{1,0:T(8,128)(2,1)} %v_hbm.1, f32[16,128]{1,0:T(8,128)} %bitcast.3, s32[3,4096]{1,0:T(4,128)} %index_hbm.1, f32[1,4096]{1,0:T(1,128)} %bitcast.2), custom_call_target="tpu_custom_call" | custom-call | tf_op jit(solution)/shard_map/muffin_tin/pallas_call | solution.py:363
  43.5 0.7 %copy.9 = f32[162,162]{1,0:T(8,128)} copy(f32[162,162]{1,0:T(8,128)S(1)} %get-tuple-element.2) | data formatting | bytes 209952
  44.1 0.6 %copy.10 = f32[4,81]{1,0:T(4,128)} copy(f32[4,81]{1,0:T(4,128)S(1)} %get-tuple-element.3) | data formatting | bytes 2592
